TPU v7x, 32 devices: a whole 2x2x4 slice. The times are simulated.
32 devices in a mesh: lon: 8 (over y, x, core), lat: 4 (over z).
Axes of the slice: x: 2, y: 2, z: 4, core: 2. Of those that a mesh axis runs over, the one named last changes fastest.
Arguments:
- fields: bfloat16 [4, 128, 32, 1024], P(None, None, 'lat', 'lon'), may hold values from -12 to 12
- bracket: int32 [32, 32, 1024], P(None, 'lat', 'lon'), may hold values from 0 to 126, as said below
- fraction: bfloat16 [32, 32, 1024], P(None, 'lat', 'lon'), may hold values from 0 to 1
Outputs:
- on_pressure: bfloat16 [4, 32, 32, 1024], P(None, None, ('lat', 'lon'))
- zonal_mean: float32 [4, 32, 32], P(None, None, ('lat', 'lon'))
- meridional: float32 [4, 32, 32], P(None, None, ('lat', 'lon'))
Inputs may be any that keep to these rules, and one draw needn't show every extreme that they name: bracket[p, r, c] - min(p * 4, 112) lies in 0 to 14 for every column, and each of these offsets occurs.
All inputs are finite; a program needn't handle non-finite values.
Results may differ from a plain program's by a relative error of at most 0.0012.
Values may be sent and summed in bfloat16 or wider, within the bound.
A program may use at most 128 MiB of HBM per device.

v0:
```python
import functools

import jax
import jax.numpy as jnp
from jax import lax
from jax.experimental import pallas as pl
from jax.experimental.pallas import tpu as pltpu
from jax.sharding import PartitionSpec as P

WINDOW = 16
TILE = 8
MESH = pl.DeviceIdType.MESH


def select_pair(levels, masks):
    bit = len(levels) // 2
    for mask in masks:
        levels = [
            jnp.where(mask, levels[k + bit], levels[k]) if k + bit < len(levels) else levels[k]
            for k in range(bit + 1)
        ]
        bit //= 2
    return levels


def exchange(
    lon_count, lat_count, fields_hbm, bracket_hbm, fraction_hbm,
    out_ref, sums, cross_lo, cross_hi,
    fields, bracket, fraction, send,
    in_sem, field_sem, own_sem, send_sem, recv_sem, sum_send, sum_recv,
    cross_send, lo_recv, hi_recv,
):
    var_count, level_count, row_count, lons = fields.shape
    plev_count = bracket.shape[0]
    own = row_count // lon_count
    group_size = min(TILE, plev_count)
    level_step = level_count // plev_count
    me = lax.axis_index("lon")
    band = lax.axis_index("lat")
    next_band = (band + 1) % lat_count
    prev_band = (band + lat_count - 1) % lat_count
    has_lo = jnp.logical_and(me == 0, band > 0)
    has_hi = jnp.logical_and(me == lon_count - 1, band < lat_count - 1)
    my_lons = pl.ds(pl.multiple_of(me * lons, 128), lons)

    get_bracket = pltpu.make_async_copy(bracket_hbm, bracket, in_sem.at[0])
    get_fraction = pltpu.make_async_copy(fraction_hbm, fraction, in_sem.at[1])

    def get_fields(v):
        return pltpu.make_async_copy(fields_hbm.at[v], fields.at[v], field_sem.at[v])

    get_bracket.start()
    get_fraction.start()
    for v in range(var_count):
        get_fields(v).start()

    barrier = pltpu.get_barrier_semaphore()
    for step in range(1, lon_count):
        peer = (me + step) % lon_count
        pl.semaphore_signal(barrier, inc=1, device_id={"lon": peer}, device_id_type=MESH)

    @pl.when(has_lo)
    def _():
        for l in range(lon_count):
            pl.semaphore_signal(barrier, inc=1, device_id={"lon": l, "lat": prev_band}, device_id_type=MESH)

    @pl.when(has_hi)
    def _():
        for l in range(lon_count):
            pl.semaphore_signal(barrier, inc=1, device_id={"lon": l, "lat": next_band}, device_id_type=MESH)

    def block_copy(v, step):
        peer = (me + step) % lon_count
        return pltpu.make_async_remote_copy(
            src_ref=send.at[v, pl.ds(peer * own, own)],
            dst_ref=out_ref.at[v, :, :, my_lons],
            send_sem=send_sem.at[step],
            recv_sem=recv_sem.at[step],
            device_id={"lon": peer},
            device_id_type=MESH,
        )

    def own_copy(v):
        return pltpu.make_async_copy(
            send.at[v, pl.ds(me * own, own)], out_ref.at[v, :, :, my_lons], own_sem.at[v]
        )

    def sum_copy(step):
        return pltpu.make_async_remote_copy(
            src_ref=sums.at[me],
            dst_ref=sums.at[me],
            send_sem=sum_send.at[step],
            recv_sem=sum_recv.at[step],
            device_id={"lon": (me + step) % lon_count},
            device_id_type=MESH,
        )

    def up_copy():
        return pltpu.make_async_remote_copy(
            src_ref=sums.at[me], dst_ref=cross_lo.at[me],
            send_sem=cross_send.at[0], recv_sem=lo_recv.at[me],
            device_id={"lon": 0, "lat": next_band}, device_id_type=MESH,
        )

    def down_copy():
        return pltpu.make_async_remote_copy(
            src_ref=sums.at[me], dst_ref=cross_hi.at[me],
            send_sem=cross_send.at[1], recv_sem=hi_recv.at[me],
            device_id={"lon": lon_count - 1, "lat": prev_band}, device_id_type=MESH,
        )

    get_bracket.wait()
    get_fraction.wait()
    ones = jnp.ones((TILE, lons), jnp.bfloat16)

    @pl.loop(0, var_count)
    def _(v):
        get_fields(v).wait()

        @pl.loop(0, row_count // TILE)
        def _(tile):
            rows = pl.ds(pl.multiple_of(tile * TILE, TILE), TILE)
            loaded, group = {}, []
            for p in range(plev_count):
                base = min(p * level_step, level_count - WINDOW)
                for k in range(base, base + WINDOW):
                    if k not in loaded:
                        loaded[k] = fields[v, k, rows, :].astype(jnp.float32)
                offset = bracket[p, rows, :] - base
                masks, bit = [], WINDOW // 2
                while bit:
                    masks.append((offset & bit) != 0)
                    bit //= 2
                lower, upper = select_pair([loaded[base + k] for k in range(WINDOW)], masks)
                weight = fraction[p, rows, :].astype(jnp.float32)
                group.append(lower + weight * (upper - lower))
                if len(group) == group_size:
                    by_row = jnp.transpose(jnp.stack(group), (1, 0, 2)).astype(jnp.bfloat16)
                    send[v, rows, p + 1 - group_size : p + 1, :] = by_row
                    group = []
            rounded = send[v, rows].reshape(TILE * plev_count, lons)
            total = lax.dot_general(
                ones, rounded, (((1,), (1,)), ((), ())), preferred_element_type=jnp.float32
            )
            width = TILE * plev_count
            sums[me, v, :, pl.ds(pl.multiple_of(tile * width, width), width)] = total[0:1]

        @pl.when(v == 0)
        def _():
            beyond = (band < lat_count - 1).astype(jnp.int32) + (band > 0).astype(jnp.int32)
            pl.semaphore_wait(barrier, lon_count - 1 + beyond)

        for step in range(lon_count - 1, 0, -1):
            block_copy(v, step).start()
        own_copy(v).start()

    @pl.when(band < lat_count - 1)
    def _():
        up_copy().start()

    @pl.when(band > 0)
    def _():
        down_copy().start()

    for step in range(1, lon_count):
        sum_copy(step).start()

    for step in range(1, lon_count):
        sum_copy(step).wait_recv()

    @pl.when(has_lo)
    def _():
        for l in range(lon_count):
            pltpu.make_async_copy(cross_lo.at[l], cross_lo.at[l], lo_recv.at[l]).wait()

    @pl.when(has_hi)
    def _():
        for l in range(lon_count):
            pltpu.make_async_copy(cross_hi.at[l], cross_hi.at[l], hi_recv.at[l]).wait()

    for v in range(var_count):
        own_copy(v).wait()
    for step in range(1, lon_count):
        source = (me + lon_count - step) % lon_count
        landed = out_ref.at[:, :, :, pl.ds(pl.multiple_of(source * lons, 128), lons)]
        pltpu.make_async_copy(landed, landed, recv_sem.at[step]).wait()
    for step in range(1, lon_count):
        peer = (me + step) % lon_count
        left = send.at[:, pl.ds(peer * own, own)]
        pltpu.make_async_copy(left, left, send_sem.at[step]).wait()
        sum_copy(step).wait_send()

    @pl.when(band < lat_count - 1)
    def _():
        up_copy().wait_send()

    @pl.when(band > 0)
    def _():
        down_copy().wait_send()


def finish(
    lon_count, lat_count, count, rows_vmem, sums, cross_lo, cross_hi,
    out_hbm, zonal_hbm, merid_hbm, zonal, merid, sem,
):
    var_count, own, plev_count = zonal.shape
    row_count = own * lon_count
    me = lax.axis_index("lon")
    band = lax.axis_index("lat")
    has_lo = jnp.logical_and(me == 0, band > 0)
    has_hi = jnp.logical_and(me == lon_count - 1, band < lat_count - 1)
    put_rows = pltpu.make_async_copy(rows_vmem, out_hbm, sem.at[0])
    put_rows.start()

    mean = sums[0]
    for l in range(1, lon_count):
        mean = mean + sums[l]
    mean = mean / count
    width = row_count * plev_count

    def row_of(q):
        shift = (2 * width - q * plev_count) % width
        return pltpu.roll(mean.reshape(var_count, width), shift, 1)[:, :plev_count]

    def edge(cross, row):
        total = cross[0]
        for l in range(1, lon_count):
            total = total + cross[l]
        total = (total / count).reshape(var_count, width)
        return total[:, row * plev_count : (row + 1) * plev_count]

    first = me * own
    for j in range(own):
        here = row_of(first + j)
        below = row_of(first + j - 1)
        above = row_of(first + j + 1)
        zonal[:, j, :] = here
        lower_edge = jnp.logical_and(first + j == 0, band == 0)
        upper_edge = jnp.logical_and(first + j == row_count - 1, band == lat_count - 1)
        below = jnp.where(lower_edge, here, below)
        above = jnp.where(upper_edge, here, above)
        scale = jnp.where(jnp.logical_or(lower_edge, upper_edge), 1.0, 0.5)
        merid[:, j, :] = scale * (above - below)

    @pl.when(has_lo)
    def _():
        below = edge(cross_lo, row_count - 1)
        above = row_of(jnp.int32(1))
        merid[:, 0, :] = 0.5 * (above - below)

    @pl.when(has_hi)
    def _():
        above = edge(cross_hi, 0)
        below = row_of(jnp.int32(row_count - 2))
        merid[:, own - 1, :] = 0.5 * (above - below)

    put_zonal = pltpu.make_async_copy(zonal, zonal_hbm, sem.at[1])
    put_merid = pltpu.make_async_copy(merid, merid_hbm, sem.at[2])
    put_zonal.start()
    put_merid.start()
    put_rows.wait()
    put_zonal.wait()
    put_merid.wait()


def shards(lon_count, lat_count, fields, bracket, fraction):
    var_count, level_count, row_count, lons = fields.shape
    plev_count = bracket.shape[0]
    own = row_count // lon_count
    sum_shape = (lon_count, var_count, 1, row_count * plev_count)
    dma = pltpu.SemaphoreType.DMA
    anywhere = pl.BlockSpec(memory_space=pl.ANY)
    room = 2 * fields.size + 4 * bracket.size + 2 * fraction.size * (1 + var_count)
    in_vmem = pl.BlockSpec(memory_space=pltpu.VMEM)
    rows_shape = (var_count, own, plev_count, lons * lon_count)
    inputs = [pltpu.with_memory_space_constraint(x, pltpu.HBM) for x in (fields, bracket, fraction)]
    held = pl.pallas_call(
        functools.partial(exchange, lon_count, lat_count),
        out_shape=(
            pltpu.VMEM(rows_shape, jnp.bfloat16),
            pltpu.VMEM(sum_shape, jnp.float32),
            pltpu.VMEM(sum_shape, jnp.float32),
            pltpu.VMEM(sum_shape, jnp.float32),
        ),
        in_specs=[anywhere] * 3,
        out_specs=(in_vmem,) * 4,
        scratch_shapes=[
            pltpu.VMEM(fields.shape, fields.dtype),
            pltpu.VMEM(bracket.shape, bracket.dtype),
            pltpu.VMEM(fraction.shape, fraction.dtype),
            pltpu.VMEM((var_count, row_count, plev_count, lons), jnp.bfloat16),
            dma((2,)),
            dma((var_count,)),
            dma((var_count,)),
            dma((lon_count,)),
            dma((lon_count,)),
            dma((lon_count,)),
            dma((lon_count,)),
            dma((2,)),
            dma((lon_count,)),
            dma((lon_count,)),
        ],
        compiler_params=pltpu.CompilerParams(
            collective_id=0, has_side_effects=True, vmem_limit_bytes=room + (8 << 20)
        ),
    )(*inputs)
    held = [pltpu.with_memory_space_constraint(x, pltpu.VMEM) for x in held]
    mean_shape = (var_count, own, plev_count)
    on_pressure, zonal_mean, meridional = pl.pallas_call(
        functools.partial(finish, lon_count, lat_count, float(lons * lon_count)),
        out_shape=(
            jax.ShapeDtypeStruct(rows_shape, jnp.bfloat16),
            jax.ShapeDtypeStruct(mean_shape, jnp.float32),
            jax.ShapeDtypeStruct(mean_shape, jnp.float32),
        ),
        in_specs=[in_vmem] * 4,
        out_specs=(anywhere,) * 3,
        scratch_shapes=[
            pltpu.VMEM(mean_shape, jnp.float32),
            pltpu.VMEM(mean_shape, jnp.float32),
            dma((3,)),
        ],
        compiler_params=pltpu.CompilerParams(vmem_limit_bytes=8 << 20),
    )(*held)
    return (
        on_pressure.transpose(0, 2, 1, 3),
        zonal_mean.transpose(0, 2, 1),
        meridional.transpose(0, 2, 1),
    )


def solution(mesh):
    return jax.shard_map(
        functools.partial(shards, mesh.shape["lon"], mesh.shape["lat"]),
        mesh=mesh,
        in_specs=(P(None, None, "lat", "lon"), P(None, "lat", "lon"), P(None, "lat", "lon")),
        out_specs=(
            P(None, None, ("lat", "lon"), None),
            P(None, None, ("lat", "lon")),
            P(None, None, ("lat", "lon")),
        ),
        check_vma=False,
    )
```

profile of v0, /device:TPU:0, one launch (start us, length us, event | category | flops | bytes accessed | tf_op | source)
XLA Modules:
  0.0 11.6 jit_solution(16311650409287398779)
XLA Ops:
  0.6 10.2 %shard_map.58 = (bf16[4,1,32,1024]{3,2,1,0:T(8,128)(2,1)S(1)}, f32[8,4,1,256]{3,2,1,0:T(1,128)S(1)}, f32[8,4,1,256]{3,2,1,0:T(1,128)S(1)}, f32[8,4,1,256]{3,2,1,0:T(1,128)S(1)}) custom-call(bf16[4,128,8,128]{3,2,1,0:T(8,128)(2,1)} %fields_hbm.1, s32[32,8,128]{2,1,0:T(8,128)} %bracket_hbm.1, bf16[32,8,128]{2,1,0:T(8,128)(2,1)} %fraction_hbm.1), custom_call_target="tpu_custom_call" | custom-call | tf_op jit(solution)/shard_map/pallas_call | solution.py:277
  10.8 0.8 %shard_map.59 = (bf16[4,1,32,1024]{3,2,1,0:T(8,128)(2,1)}, f32[4,1,32]{2,1,0:T(1,128)}, f32[4,1,32]{2,1,0:T(1,128)}) custom-call(bf16[4,1,32,1024]{3,2,1,0:T(8,128)(2,1)S(1)} %get-tuple-element.10.rows_vmem, f32[8,4,1,256]{3,2,1,0:T(1,128)S(1)} %get-tuple-element.11.sums, f32[8,4,1,256]{3,2,1,0:T(1,128)S(1)} %get-tuple-element.12.cross_lo, ...), custom_call_target="tpu_custom_call" | custom-call | tf_op jit(solution)/shard_map/pallas_call | solution.py:309
where the time goes:
time: 11.7 us; the launch traced here: 11.6 us
  Pallas kernels  10.9 us (93%)
  between operations  0.64 us (5%)
    pallas_call x1, Pallas kernels, shards(): pl.pallas_call(functools.partial(exchange, lon_count, lat_count), out_sha...  10.2 us
    pallas_call x1, Pallas kernels, shards(): pl.pallas_call(functools.partial(finish, lon_count, lat_count, float(lons...  0.76 us

commit v1 on v0

v1 whole, which is shorter than its diff:
```python
import functools

import jax
import jax.numpy as jnp
from jax import lax
from jax.experimental import pallas as pl
from jax.experimental.pallas import tpu as pltpu
from jax.sharding import PartitionSpec as P

WINDOW = 16
TILE = 8
PACK = 16
MESH = pl.DeviceIdType.MESH
HUB = 2


def select_pair(levels, masks):
    bit = len(levels) // 2
    for mask in masks:
        levels = [
            jnp.where(mask, levels[k + bit], levels[k]) if k + bit < len(levels) else levels[k]
            for k in range(bit + 1)
        ]
        bit //= 2
    return levels


def partner(me, k, count):
    if count & (count - 1):
        return (me + k) % count, (me + count - k) % count
    peer, bit = me, 1
    while bit < count:
        if k & bit:
            peer = peer + bit - 2 * bit * ((me // bit) % 2)
        bit *= 2
    return peer, peer


def interpolate(pair, fields, bracket, fraction, send):
    _, level_count, both_rows, lons = fields.shape
    plev_count, row_count, _ = bracket.shape
    level_step = level_count // plev_count
    group_size = min(TILE, plev_count)

    def block(tile):
        where = [tile * PACK + half for half in range(0, PACK, TILE)]
        rows = [pl.ds(pl.multiple_of(at % row_count, TILE), TILE) for at in where]
        packed = pl.ds(pl.multiple_of(tile * PACK, PACK), PACK)
        loaded, groups = {}, [[], []]
        for p in range(plev_count):
            base = min(p * level_step, level_count - WINDOW)
            for k in range(base, base + WINDOW):
                if k not in loaded:
                    loaded[k] = fields[pair, k, packed, :]
            offset = (jnp.concatenate([bracket[p, r, :] for r in rows]) - base).astype(jnp.int16)
            masks, bit = [], WINDOW // 2
            while bit:
                masks.append((offset & jnp.int16(bit)) != jnp.int16(0))
                bit //= 2
            lower, upper = select_pair([loaded[base + k] for k in range(WINDOW)], masks)
            lower, upper = lower.astype(jnp.float32), upper.astype(jnp.float32)
            weight = jnp.concatenate([fraction[p, r, :] for r in rows]).astype(jnp.float32)
            value = lower + weight * (upper - lower)
            groups[0].append(value[:TILE])
            groups[1].append(value[TILE:])
            if len(groups[0]) == group_size:
                for half in range(2):
                    by_row = jnp.transpose(jnp.stack(groups[half]), (1, 0, 2)).astype(jnp.bfloat16)
                    v = 2 * pair + where[half] // row_count
                    send[v, rows[half], p + 1 - group_size : p + 1, :] = by_row
                groups = [[], []]

    if both_rows == PACK:
        block(0)
    else:
        pl.loop(0, both_rows // PACK)(block)


def exchange(
    lon_count, lat_count, count, fields_hbm, bracket_hbm, fraction_hbm,
    out_ref, zonal, merid,
    fields, bracket, fraction, send, sums, got, cross,
    in_sem, field_sem, send_sem, recv_sem, sum_send, sum_recv, edge_send, edge_recv,
):
    var_count, row_count, plev_count, lons = send.shape
    pair_count = var_count // 2
    own = row_count // lon_count
    width = var_count * plev_count
    me = lax.axis_index("lon")
    band = lax.axis_index("lat")
    next_band = (band + 1) % lat_count
    prev_band = (band + lat_count - 1) % lat_count
    first = me == 0
    last = me == lon_count - 1
    up = band < lat_count - 1
    down = band > 0
    my_lons = pl.ds(pl.multiple_of(me * lons, 128), lons)
    peers = [partner(me, k, lon_count)[0] for k in range(lon_count - 1, 0, -1)]

    barrier = pltpu.get_barrier_semaphore()
    for peer in peers:
        pl.semaphore_signal(barrier, inc=1, device_id={"lon": peer}, device_id_type=MESH)

    @pl.when(jnp.logical_and(first, down))
    def _():
        for l in range(lon_count):
            pl.semaphore_signal(barrier, inc=1, device_id={"lon": l, "lat": prev_band}, device_id_type=MESH)

    @pl.when(jnp.logical_and(last, up))
    def _():
        for l in range(lon_count):
            pl.semaphore_signal(barrier, inc=1, device_id={"lon": l, "lat": next_band}, device_id_type=MESH)

    get_bracket = pltpu.make_async_copy(bracket_hbm, bracket, in_sem.at[0])
    get_fraction = pltpu.make_async_copy(fraction_hbm, fraction, in_sem.at[1])
    get_bracket.start()
    get_fraction.start()
    for v in range(var_count):
        pltpu.make_async_copy(
            fields_hbm.at[v],
            fields.at[v // 2, :, pl.ds(v % 2 * row_count, row_count)],
            field_sem.at[v // 2],
        ).start()

    def send_block(peer, pair):
        some = pl.ds(2 * pair, 2)
        pltpu.make_async_remote_copy(
            src_ref=send.at[some, pl.ds(peer * own, own)],
            dst_ref=out_ref.at[some, :, :, my_lons],
            send_sem=send_sem.at[0],
            recv_sem=recv_sem.at[0],
            device_id={"lon": peer},
            device_id_type=MESH,
        ).start()

    def send_sums(peer):
        pltpu.make_async_remote_copy(
            src_ref=sums.at[pl.ds(peer * own, own + 2)],
            dst_ref=got.at[me],
            send_sem=sum_send.at[0],
            recv_sem=sum_recv.at[0],
            device_id={"lon": peer},
            device_id_type=MESH,
        ).start()

    def send_edge(row, lon, lat):
        pltpu.make_async_remote_copy(
            src_ref=sums.at[row],
            dst_ref=cross.at[me],
            send_sem=edge_send.at[0],
            recv_sem=edge_recv.at[0],
            device_id={"lon": lon, "lat": lat},
            device_id_type=MESH,
        ).start()

    def to_hubs(go, *args):
        for h in range(HUB):
            pl.when(me != h)(functools.partial(go, h, *args))

    def to_others(go, *args):
        for peer in peers:
            pl.when(peer >= HUB)(functools.partial(go, peer, *args))

    sums[0] = jnp.zeros((1, width), jnp.float32)
    sums[row_count + 1] = jnp.zeros((1, width), jnp.float32)
    get_bracket.wait()
    get_fraction.wait()
    for pair in range(pair_count):
        pltpu.make_async_copy(fields.at[pair], fields.at[pair], field_sem.at[pair]).wait()
        interpolate(pair, fields, bracket, fraction, send)
        if pair == 0:
            beyond = up.astype(jnp.int32) + down.astype(jnp.int32)
            pl.semaphore_wait(barrier, lon_count - 1 + beyond)
        if pair < pair_count - 1:
            to_hubs(send_block, pair)

    ones = jnp.ones((TILE, lons), jnp.bfloat16)

    def add_up(at):
        two = jnp.concatenate([send[:, at + r].reshape(width, lons) for r in range(2)])
        total = lax.dot_general(
            ones, two, (((1,), (1,)), ((), ())), preferred_element_type=jnp.float32
        )
        sums[at + 1] = total[0:1, :width]
        sums[at + 2] = total[0:1, width:]

    if row_count == TILE:
        for at in range(0, row_count, 2):
            add_up(at)
    else:
        pl.loop(0, row_count // 2)(lambda half: add_up(2 * half))

    to_hubs(send_sums)
    to_others(send_sums)
    pl.when(up)(lambda: send_edge(row_count, 0, next_band))
    pl.when(down)(lambda: send_edge(1, lon_count - 1, prev_band))
    to_hubs(send_block, pair_count - 1)
    for pair in range(pair_count):
        to_others(send_block, pair)

    out_ref[:, :, :, my_lons] = send[:, pl.ds(me * own, own)]
    got[me] = sums[pl.ds(me * own, own + 2)]
    all_sums = got.at[pl.ds(0, lon_count - 1)]
    pltpu.make_async_copy(all_sums, all_sums, sum_recv.at[0]).wait()

    def mean_of(parts):
        total = parts[0]
        for part in parts[1:]:
            total = total + part
        return total / count

    here = [mean_of([got[l, j] for l in range(lon_count)]) for j in range(own + 2)]
    for j in range(own):
        for v in range(var_count):
            zonal[v, j : j + 1, :] = here[j + 1][:, v * plev_count : (v + 1) * plev_count]

    @pl.when(jnp.logical_or(jnp.logical_and(first, down), jnp.logical_and(last, up)))
    def _():
        pltpu.make_async_copy(cross, cross, edge_recv.at[0]).wait()

    beyond_edge = mean_of([cross[l] for l in range(lon_count)])
    bottom = jnp.logical_and(first, band == 0)
    top = jnp.logical_and(last, band == lat_count - 1)
    for j in range(own):
        below, middle, above = here[j : j + 3]
        scale = jnp.float32(0.5)
        if j == 0:
            below = jnp.where(bottom, middle, jnp.where(first, beyond_edge, below))
            scale = jnp.where(bottom, 1.0, scale)
        if j == own - 1:
            above = jnp.where(top, middle, jnp.where(last, beyond_edge, above))
            scale = jnp.where(top, 1.0, scale)
        slope = scale * (above - below)
        for v in range(var_count):
            merid[v, j : j + 1, :] = slope[:, v * plev_count : (v + 1) * plev_count]

    pltpu.make_async_copy(all_sums, all_sums, sum_send.at[0]).wait()

    @pl.when(jnp.logical_and(up, down))
    def _():
        two = sums.at[pl.ds(0, 2)]
        pltpu.make_async_copy(two, two, edge_send.at[0]).wait()

    @pl.when(up != down)
    def _():
        one = sums.at[pl.ds(0, 1)]
        pltpu.make_async_copy(one, one, edge_send.at[0]).wait()

    landed = out_ref.at[:, :, :, pl.ds(0, (lon_count - 1) * lons)]
    pltpu.make_async_copy(landed, landed, recv_sem.at[0]).wait()
    left = send.at[:, pl.ds(0, row_count - own)]
    pltpu.make_async_copy(left, left, send_sem.at[0]).wait()


def finish(rows_vmem, zonal_vmem, merid_vmem, out_hbm, zonal_hbm, merid_hbm, sem):
    puts = [
        pltpu.make_async_copy(rows_vmem, out_hbm, sem.at[0]),
        pltpu.make_async_copy(zonal_vmem, zonal_hbm, sem.at[1]),
        pltpu.make_async_copy(merid_vmem, merid_hbm, sem.at[2]),
    ]
    for put in puts:
        put.start()
    for put in puts:
        put.wait()


def shards(lon_count, lat_count, fields, bracket, fraction):
    var_count, level_count, row_count, lons = fields.shape
    plev_count = bracket.shape[0]
    own = row_count // lon_count
    width = var_count * plev_count
    dma = pltpu.SemaphoreType.DMA
    anywhere = pl.BlockSpec(memory_space=pl.ANY)
    room = 2 * fields.size + 4 * bracket.size + 2 * fraction.size * (1 + var_count)
    in_vmem = pl.BlockSpec(memory_space=pltpu.VMEM)
    rows_shape = (var_count, own, plev_count, lons * lon_count)
    mean_shape = (var_count, own, plev_count)
    inputs = [pltpu.with_memory_space_constraint(x, pltpu.HBM) for x in (fields, bracket, fraction)]
    held = pl.pallas_call(
        functools.partial(exchange, lon_count, lat_count, float(lons * lon_count)),
        out_shape=(
            pltpu.VMEM(rows_shape, jnp.bfloat16),
            pltpu.VMEM(mean_shape, jnp.float32),
            pltpu.VMEM(mean_shape, jnp.float32),
        ),
        in_specs=[anywhere] * 3,
        out_specs=(in_vmem,) * 3,
        scratch_shapes=[
            pltpu.VMEM((var_count // 2, level_count, 2 * row_count, lons), fields.dtype),
            pltpu.VMEM(bracket.shape, bracket.dtype),
            pltpu.VMEM(fraction.shape, fraction.dtype),
            pltpu.VMEM((var_count, row_count, plev_count, lons), jnp.bfloat16),
            pltpu.VMEM((row_count + 2, 1, width), jnp.float32),
            pltpu.VMEM((lon_count, own + 2, 1, width), jnp.float32),
            pltpu.VMEM((lon_count, 1, width), jnp.float32),
            dma((2,)),
            dma((var_count // 2,)),
            dma((1,)),
            dma((1,)),
            dma((1,)),
            dma((1,)),
            dma((1,)),
            dma((1,)),
        ],
        compiler_params=pltpu.CompilerParams(
            collective_id=0, has_side_effects=True, vmem_limit_bytes=room + (8 << 20)
        ),
    )(*inputs)
    held = [pltpu.with_memory_space_constraint(x, pltpu.VMEM) for x in held]
    on_pressure, zonal_mean, meridional = pl.pallas_call(
        finish,
        out_shape=(
            jax.ShapeDtypeStruct(rows_shape, jnp.bfloat16),
            jax.ShapeDtypeStruct(mean_shape, jnp.float32),
            jax.ShapeDtypeStruct(mean_shape, jnp.float32),
        ),
        in_specs=[in_vmem] * 3,
        out_specs=(anywhere,) * 3,
        scratch_shapes=[dma((3,))],
        compiler_params=pltpu.CompilerParams(vmem_limit_bytes=8 << 20),
    )(*held)
    return (
        on_pressure.transpose(0, 2, 1, 3),
        zonal_mean.transpose(0, 2, 1),
        meridional.transpose(0, 2, 1),
    )


def solution(mesh):
    return jax.shard_map(
        functools.partial(shards, mesh.shape["lon"], mesh.shape["lat"]),
        mesh=mesh,
        in_specs=(P(None, None, "lat", "lon"), P(None, "lat", "lon"), P(None, "lat", "lon")),
        out_specs=(
            P(None, None, ("lat", "lon"), None),
            P(None, None, ("lat", "lon")),
            P(None, None, ("lat", "lon")),
        ),
        check_vma=False,
    )
```

time: 11.7 us -> 9.9 us (0.85)
  Pallas kernels: 10.9 us -> 9.11 us
    pallas_call x2, Pallas kernels: 10.9 us -> 9.11 us  [the longest x1 8.38 us: shards(): pl.pallas_call(functools.partial(exchange, lon_count, lat_count, float(lo...]
where the time goes in v1:
time: 9.9 us; the launch traced here: 9.75 us
  Pallas kernels  9.11 us (92%)
  between operations  0.64 us (6%)
    pallas_call x1, Pallas kernels, shards(): pl.pallas_call(functools.partial(exchange, lon_count, lat_count, float(lo...  8.38 us
    pallas_call x1, Pallas kernels, shards(): pl.pallas_call(finish, out_shape=(jax.ShapeDtypeStruct(rows_shape, jnp.bf...  0.74 us

profile of v1, /device:TPU:0, one launch (start us, length us, event | category | flops | bytes accessed | tf_op | source)
XLA Modules:
  0.0 9.8 jit_solution(12184774696222139777)
XLA Ops:
  0.6 8.4 %shard_map.58 = (bf16[4,1,32,1024]{3,2,1,0:T(8,128)(2,1)S(1)}, f32[4,1,32]{2,1,0:T(1,128)S(1)}, f32[4,1,32]{2,1,0:T(1,128)S(1)}) custom-call(bf16[4,128,8,128]{3,2,1,0:T(8,128)(2,1)} %fields_hbm.1, s32[32,8,128]{2,1,0:T(8,128)} %bracket_hbm.1, bf16[32,8,128]{2,1,0:T(8,128)(2,1)} %fraction_hbm.1), custom_call_target="tpu_custom_call" | custom-call | tf_op jit(solution)/shard_map/pallas_call | solution.py:279
  9.0 0.7 %shard_map.59 = (bf16[4,1,32,1024]{3,2,1,0:T(8,128)(2,1)}, f32[4,1,32]{2,1,0:T(1,128)}, f32[4,1,32]{2,1,0:T(1,128)}) custom-call(bf16[4,1,32,1024]{3,2,1,0:T(8,128)(2,1)S(1)} %get-tuple-element.9.rows_vmem, f32[4,1,32]{2,1,0:T(1,128)S(1)} %get-tuple-element.10.zonal_vmem, f32[4,1,32]{2,1,0:T(1,128)S(1)} %get-tuple-element.11.merid_vmem), custom_call_target="tpu_custom_call" | custom-call | tf_op jit(solution)/shard_map/pallas_call | solution.py:310

commit v2 on v1

--- a/solution.py
+++ b/solution.py
@@ -1,4 +1,5 @@
 import functools
+import math
 
 import jax
 import jax.numpy as jnp
@@ -12,6 +13,7 @@
 PACK = 16
 MESH = pl.DeviceIdType.MESH
 HUB = 2
+PARTS = (2, 2)
 
 
 def select_pair(levels, masks):
@@ -36,7 +38,7 @@
     return peer, peer
 
 
-def interpolate(pair, fields, bracket, fraction, send):
+def interpolate(pair, levels, fields, bracket, fraction, send):
     _, level_count, both_rows, lons = fields.shape
     plev_count, row_count, _ = bracket.shape
     level_step = level_count // plev_count
@@ -47,7 +49,7 @@
         rows = [pl.ds(pl.multiple_of(at % row_count, TILE), TILE) for at in where]
         packed = pl.ds(pl.multiple_of(tile * PACK, PACK), PACK)
         loaded, groups = {}, [[], []]
-        for p in range(plev_count):
+        for p in levels:
             base = min(p * level_step, level_count - WINDOW)
             for k in range(base, base + WINDOW):
                 if k not in loaded:
@@ -80,7 +82,7 @@
     lon_count, lat_count, count, fields_hbm, bracket_hbm, fraction_hbm,
     out_ref, zonal, merid,
     fields, bracket, fraction, send, sums, got, cross,
-    in_sem, field_sem, send_sem, recv_sem, sum_send, sum_recv, edge_send, edge_recv,
+    in_sem, field_sem, send_sem, recv_sem, sum_send, sum_recv, edge_send, edge_recv, go,
 ):
     var_count, row_count, plev_count, lons = send.shape
     pair_count = var_count // 2
@@ -95,38 +97,56 @@
     up = band < lat_count - 1
     down = band > 0
     my_lons = pl.ds(pl.multiple_of(me * lons, 128), lons)
-    peers = [partner(me, k, lon_count)[0] for k in range(lon_count - 1, 0, -1)]
-
-    barrier = pltpu.get_barrier_semaphore()
-    for peer in peers:
-        pl.semaphore_signal(barrier, inc=1, device_id={"lon": peer}, device_id_type=MESH)
-
-    @pl.when(jnp.logical_and(first, down))
-    def _():
-        for l in range(lon_count):
-            pl.semaphore_signal(barrier, inc=1, device_id={"lon": l, "lat": prev_band}, device_id_type=MESH)
-
-    @pl.when(jnp.logical_and(last, up))
-    def _():
-        for l in range(lon_count):
-            pl.semaphore_signal(barrier, inc=1, device_id={"lon": l, "lat": next_band}, device_id_type=MESH)
+    steps = range(lon_count - 1, 0, -1)
+    peers = [partner(me, k, lon_count)[0] for k in steps]
+    others = [(peer, (me // 2) % 2 != (k // 2) % 2) for k, peer in zip(steps, peers)]
+    hub = me < HUB
+    far = me >= lon_count - 2
+    late = jnp.logical_and(me % 2 == 1, jnp.logical_not(jnp.logical_or(hub, far)))
+    early = jnp.logical_or(far, late)
+    full = jnp.logical_not(early)
 
     get_bracket = pltpu.make_async_copy(bracket_hbm, bracket, in_sem.at[0])
     get_fraction = pltpu.make_async_copy(fraction_hbm, fraction, in_sem.at[1])
     get_bracket.start()
     get_fraction.start()
-    for v in range(var_count):
-        pltpu.make_async_copy(
-            fields_hbm.at[v],
-            fields.at[v // 2, :, pl.ds(v % 2 * row_count, row_count)],
-            field_sem.at[v // 2],
-        ).start()
-
-    def send_block(peer, pair):
-        some = pl.ds(2 * pair, 2)
+
+    def get_pair(pair):
+        for half in range(2):
+            pltpu.make_async_copy(
+                fields_hbm.at[2 * pair + half],
+                fields.at[pair, :, pl.ds(half * row_count, row_count)],
+                field_sem.at[pair],
+            ).start()
+
+    for pair in range(pair_count):
+        get_pair(pair)
+
+    barrier = pltpu.get_barrier_semaphore()
+
+    def greet(peer, lat):
+        pl.semaphore_signal(barrier, inc=1, device_id={"lon": peer, "lat": lat}, device_id_type=MESH)
+
+    for peer in peers:
+        listens = jnp.logical_or(jnp.logical_or(hub, peer % 2 == 0), jnp.logical_or(peer < HUB, peer >= lon_count - 2))
+        pl.when(listens)(functools.partial(greet, peer, band))
+
+    waiting = [l for l in range(lon_count - 2) if l < HUB or l % 2 == 0]
+
+    @pl.when(jnp.logical_and(first, down))
+    def _():
+        for l in waiting:
+            greet(l, prev_band)
+
+    @pl.when(jnp.logical_and(last, up))
+    def _():
+        for l in waiting:
+            greet(l, next_band)
+
+    def send_block(peer, some, levels=slice(None)):
         pltpu.make_async_remote_copy(
-            src_ref=send.at[some, pl.ds(peer * own, own)],
-            dst_ref=out_ref.at[some, :, :, my_lons],
+            src_ref=send.at[some, pl.ds(peer * own, own), levels],
+            dst_ref=out_ref.at[some, :, levels, my_lons],
             send_sem=send_sem.at[0],
             recv_sem=recv_sem.at[0],
             device_id={"lon": peer},
@@ -153,26 +173,35 @@
             device_id_type=MESH,
         ).start()
 
-    def to_hubs(go, *args):
+    def to_hubs(act, *args):
         for h in range(HUB):
-            pl.when(me != h)(functools.partial(go, h, *args))
-
-    def to_others(go, *args):
+            pl.when(me != h)(functools.partial(act, h, *args))
+
+    def to_others(act, *args):
         for peer in peers:
-            pl.when(peer >= HUB)(functools.partial(go, peer, *args))
+            pl.when(peer >= HUB)(functools.partial(act, peer, *args))
 
     sums[0] = jnp.zeros((1, width), jnp.float32)
     sums[row_count + 1] = jnp.zeros((1, width), jnp.float32)
     get_bracket.wait()
     get_fraction.wait()
+    whole = pl.ds(0, var_count)
     for pair in range(pair_count):
         pltpu.make_async_copy(fields.at[pair], fields.at[pair], field_sem.at[pair]).wait()
-        interpolate(pair, fields, bracket, fraction, send)
-        if pair == 0:
-            beyond = up.astype(jnp.int32) + down.astype(jnp.int32)
-            pl.semaphore_wait(barrier, lon_count - 1 + beyond)
-        if pair < pair_count - 1:
-            to_hubs(send_block, pair)
+        some = pl.ds(2 * pair, 2)
+        parts = PARTS[pair]
+        for part in range(parts):
+            count_here = plev_count // parts
+            low = part * count_here
+            interpolate(pair, range(low, low + count_here), fields, bracket, fraction, send)
+
+            @pl.when(early)
+            def _():
+                if pair == 0 and part == 0:
+                    pl.semaphore_wait(barrier, jnp.where(far, lon_count - 1, HUB))
+                send_block(0, some, pl.ds(low, count_here))
+                if pair == 0 and part == parts - 1:
+                    pl.when(late)(functools.partial(send_block, 1, some))
 
     ones = jnp.ones((TILE, lons), jnp.bfloat16)
 
@@ -190,34 +219,72 @@
     else:
         pl.loop(0, row_count // 2)(lambda half: add_up(2 * half))
 
+    def send_edges():
+        pl.when(up)(lambda: send_edge(row_count, 0, next_band))
+        pl.when(down)(lambda: send_edge(1, lon_count - 1, prev_band))
+
+    def open_to(peer):
+        pl.semaphore_signal(go, inc=1, device_id={"lon": peer}, device_id_type=MESH)
+
+    @pl.when(full)
+    def _():
+        beyond = up.astype(jnp.int32) + down.astype(jnp.int32)
+        pl.semaphore_wait(barrier, lon_count - 1 + beyond)
+        pl.when(jnp.logical_not(hub))(lambda: open_to(me + 1))
+
+        @pl.when(me == lon_count - 4)
+        def _():
+            open_to(lon_count - 2)
+            open_to(lon_count - 1)
+
     to_hubs(send_sums)
-    to_others(send_sums)
-    pl.when(up)(lambda: send_edge(row_count, 0, next_band))
-    pl.when(down)(lambda: send_edge(1, lon_count - 1, prev_band))
-    to_hubs(send_block, pair_count - 1)
-    for pair in range(pair_count):
-        to_others(send_block, pair)
+
+    @pl.when(full)
+    def _():
+        send_edges()
+        to_others(send_sums)
+        pl.when(jnp.logical_not(first))(functools.partial(send_block, 0, whole))
+        for peer, aside in others:
+            pl.when(jnp.logical_and(peer >= HUB, aside))(functools.partial(send_block, peer, whole))
+        pl.when(me != 1)(functools.partial(send_block, 1, whole))
+        for peer, aside in others:
+            pl.when(jnp.logical_and(peer >= HUB, jnp.logical_not(aside)))(functools.partial(send_block, peer, whole))
+
+    @pl.when(early)
+    def _():
+        for pair in range(1, pair_count):
+            pl.when(late)(functools.partial(send_block, 1, pl.ds(2 * pair, 2)))
+
+        @pl.when(far)
+        def _():
+            send_block(1, whole)
+            to_others(send_sums)
+            to_others(send_block, whole)
+
+        pl.semaphore_wait(go, 1)
+        send_edges()
+
+        @pl.when(late)
+        def _():
+            to_others(send_sums)
+            to_others(send_block, whole)
 
     out_ref[:, :, :, my_lons] = send[:, pl.ds(me * own, own)]
     got[me] = sums[pl.ds(me * own, own + 2)]
     all_sums = got.at[pl.ds(0, lon_count - 1)]
     pltpu.make_async_copy(all_sums, all_sums, sum_recv.at[0]).wait()
 
+    @pl.when(jnp.logical_or(jnp.logical_and(first, down), jnp.logical_and(last, up)))
+    def _():
+        pltpu.make_async_copy(cross, cross, edge_recv.at[0]).wait()
+
     def mean_of(parts):
         total = parts[0]
         for part in parts[1:]:
             total = total + part
-        return total / count
+        return total * (1 / count) if math.frexp(count)[0] == 0.5 else total / count
 
     here = [mean_of([got[l, j] for l in range(lon_count)]) for j in range(own + 2)]
-    for j in range(own):
-        for v in range(var_count):
-            zonal[v, j : j + 1, :] = here[j + 1][:, v * plev_count : (v + 1) * plev_count]
-
-    @pl.when(jnp.logical_or(jnp.logical_and(first, down), jnp.logical_and(last, up)))
-    def _():
-        pltpu.make_async_copy(cross, cross, edge_recv.at[0]).wait()
-
     beyond_edge = mean_of([cross[l] for l in range(lon_count)])
     bottom = jnp.logical_and(first, band == 0)
     top = jnp.logical_and(last, band == lat_count - 1)
@@ -232,7 +299,9 @@
             scale = jnp.where(top, 1.0, scale)
         slope = scale * (above - below)
         for v in range(var_count):
-            merid[v, j : j + 1, :] = slope[:, v * plev_count : (v + 1) * plev_count]
+            some = slice(v * plev_count, (v + 1) * plev_count)
+            zonal[v, j : j + 1, :] = middle[:, some]
+            merid[v, j : j + 1, :] = slope[:, some]
 
     pltpu.make_async_copy(all_sums, all_sums, sum_send.at[0]).wait()
 
@@ -301,6 +370,7 @@
             dma((1,)),
             dma((1,)),
             dma((1,)),
+            pltpu.SemaphoreType.REGULAR,
         ],
         compiler_params=pltpu.CompilerParams(
             collective_id=0, has_side_effects=True, vmem_limit_bytes=room + (8 << 20)

time: 9.9 us -> 9.1 us (0.919)
  Pallas kernels: 9.11 us -> 8.31 us
    pallas_call x1, Pallas kernels: 8.38 us -> 7.58 us  [shards(): pl.pallas_call(functools.partial(exchange, lon_count, lat_count, float(lo...]
where the time goes in v2:
time: 9.1 us; the launch traced here: 8.95 us
  Pallas kernels  8.31 us (91%)
  between operations  0.64 us (7%)
    pallas_call x1, Pallas kernels, shards(): pl.pallas_call(functools.partial(exchange, lon_count, lat_count, float(lo...  7.58 us
    pallas_call x1, Pallas kernels, shards(): pl.pallas_call(finish, out_shape=(jax.ShapeDtypeStruct(rows_shape, jnp.bf...  0.74 us

profile of v2, /device:TPU:0, one launch (start us, length us, event | category | flops | bytes accessed | tf_op | source)
XLA Modules:
  0.0 8.9 jit_solution(12834685889384416805)
XLA Ops:
  0.6 7.6 %shard_map.58 = (bf16[4,1,32,1024]{3,2,1,0:T(8,128)(2,1)S(1)}, f32[4,1,32]{2,1,0:T(1,128)S(1)}, f32[4,1,32]{2,1,0:T(1,128)S(1)}) custom-call(bf16[4,128,8,128]{3,2,1,0:T(8,128)(2,1)} %fields_hbm.1, s32[32,8,128]{2,1,0:T(8,128)} %bracket_hbm.1, bf16[32,8,128]{2,1,0:T(8,128)(2,1)} %fraction_hbm.1), custom_call_target="tpu_custom_call" | custom-call | tf_op jit(solution)/shard_map/pallas_call | solution.py:348
  8.2 0.7 %shard_map.59 = (bf16[4,1,32,1024]{3,2,1,0:T(8,128)(2,1)}, f32[4,1,32]{2,1,0:T(1,128)}, f32[4,1,32]{2,1,0:T(1,128)}) custom-call(bf16[4,1,32,1024]{3,2,1,0:T(8,128)(2,1)S(1)} %get-tuple-element.9.rows_vmem, f32[4,1,32]{2,1,0:T(1,128)S(1)} %get-tuple-element.10.zonal_vmem, f32[4,1,32]{2,1,0:T(1,128)S(1)} %get-tuple-element.11.merid_vmem), custom_call_target="tpu_custom_call" | custom-call | tf_op jit(solution)/shard_map/pallas_call | solution.py:380

commit v3 on v2

--- a/solution.py
+++ b/solution.py
@@ -55,19 +55,19 @@
                 if k not in loaded:
                     loaded[k] = fields[pair, k, packed, :]
             offset = (jnp.concatenate([bracket[p, r, :] for r in rows]) - base).astype(jnp.int16)
-            masks, bit = [], WINDOW // 2
+            masks, bit = [offset >= jnp.int16(WINDOW // 2)], WINDOW // 4
             while bit:
                 masks.append((offset & jnp.int16(bit)) != jnp.int16(0))
                 bit //= 2
             lower, upper = select_pair([loaded[base + k] for k in range(WINDOW)], masks)
             lower, upper = lower.astype(jnp.float32), upper.astype(jnp.float32)
-            weight = jnp.concatenate([fraction[p, r, :] for r in rows]).astype(jnp.float32)
-            value = lower + weight * (upper - lower)
+            weight = jnp.concatenate([fraction[p, r, :].astype(jnp.float32) for r in rows])
+            value = (lower + weight * (upper - lower)).astype(jnp.bfloat16)
             groups[0].append(value[:TILE])
             groups[1].append(value[TILE:])
             if len(groups[0]) == group_size:
                 for half in range(2):
-                    by_row = jnp.transpose(jnp.stack(groups[half]), (1, 0, 2)).astype(jnp.bfloat16)
+                    by_row = jnp.transpose(jnp.stack(groups[half]), (1, 0, 2))
                     v = 2 * pair + where[half] // row_count
                     send[v, rows[half], p + 1 - group_size : p + 1, :] = by_row
                 groups = [[], []]
@@ -82,7 +82,7 @@
     lon_count, lat_count, count, fields_hbm, bracket_hbm, fraction_hbm,
     out_ref, zonal, merid,
     fields, bracket, fraction, send, sums, got, cross,
-    in_sem, field_sem, send_sem, recv_sem, sum_send, sum_recv, edge_send, edge_recv, go,
+    in_sem, field_sem, send_sem, recv_sem, sum_recv, edge_recv, go,
 ):
     var_count, row_count, plev_count, lons = send.shape
     pair_count = var_count // 2
@@ -157,7 +157,7 @@
         pltpu.make_async_remote_copy(
             src_ref=sums.at[pl.ds(peer * own, own + 2)],
             dst_ref=got.at[me],
-            send_sem=sum_send.at[0],
+            send_sem=send_sem.at[0],
             recv_sem=sum_recv.at[0],
             device_id={"lon": peer},
             device_id_type=MESH,
@@ -167,7 +167,7 @@
         pltpu.make_async_remote_copy(
             src_ref=sums.at[row],
             dst_ref=cross.at[me],
-            send_sem=edge_send.at[0],
+            send_sem=send_sem.at[0],
             recv_sem=edge_recv.at[0],
             device_id={"lon": lon, "lat": lat},
             device_id_type=MESH,
@@ -303,17 +303,17 @@
             zonal[v, j : j + 1, :] = middle[:, some]
             merid[v, j : j + 1, :] = slope[:, some]
 
-    pltpu.make_async_copy(all_sums, all_sums, sum_send.at[0]).wait()
+    pltpu.make_async_copy(all_sums, all_sums, send_sem.at[0]).wait()
 
     @pl.when(jnp.logical_and(up, down))
     def _():
         two = sums.at[pl.ds(0, 2)]
-        pltpu.make_async_copy(two, two, edge_send.at[0]).wait()
+        pltpu.make_async_copy(two, two, send_sem.at[0]).wait()
 
     @pl.when(up != down)
     def _():
         one = sums.at[pl.ds(0, 1)]
-        pltpu.make_async_copy(one, one, edge_send.at[0]).wait()
+        pltpu.make_async_copy(one, one, send_sem.at[0]).wait()
 
     landed = out_ref.at[:, :, :, pl.ds(0, (lon_count - 1) * lons)]
     pltpu.make_async_copy(landed, landed, recv_sem.at[0]).wait()
@@ -323,14 +323,16 @@
 
 def finish(rows_vmem, zonal_vmem, merid_vmem, out_hbm, zonal_hbm, merid_hbm, sem):
     puts = [
-        pltpu.make_async_copy(rows_vmem, out_hbm, sem.at[0]),
         pltpu.make_async_copy(zonal_vmem, zonal_hbm, sem.at[1]),
         pltpu.make_async_copy(merid_vmem, merid_hbm, sem.at[2]),
     ]
+    for v in range(rows_vmem.shape[0]):
+        pltpu.make_async_copy(rows_vmem.at[v], out_hbm.at[v], sem.at[0]).start()
     for put in puts:
         put.start()
     for put in puts:
         put.wait()
+    pltpu.make_async_copy(rows_vmem, out_hbm, sem.at[0]).wait()
 
 
 def shards(lon_count, lat_count, fields, bracket, fraction):
@@ -368,8 +370,6 @@
             dma((1,)),
             dma((1,)),
             dma((1,)),
-            dma((1,)),
-            dma((1,)),
             pltpu.SemaphoreType.REGULAR,
         ],
         compiler_params=pltpu.CompilerParams(

time: 9.1 us -> 9.07 us (level)
  no operation moved by 1% of the time
where the time goes in v3:
time: 9.07 us; the launch traced here: 8.92 us
  Pallas kernels  8.28 us (91%)
  between operations  0.64 us (7%)
    pallas_call x1, Pallas kernels, shards(): pl.pallas_call(functools.partial(exchange, lon_count, lat_count, float(lo...  7.56 us
    pallas_call x1, Pallas kernels, shards(): pl.pallas_call(finish, out_shape=(jax.ShapeDtypeStruct(rows_shape, jnp.bf...  0.72 us

profile of v3, /device:TPU:0, one launch (start us, length us, event | category | flops | bytes accessed | tf_op | source)
XLA Modules:
  0.0 8.9 jit_solution(1137661542265838020)
XLA Ops:
  0.6 7.6 %shard_map.58 = (bf16[4,1,32,1024]{3,2,1,0:T(8,128)(2,1)S(1)}, f32[4,1,32]{2,1,0:T(1,128)S(1)}, f32[4,1,32]{2,1,0:T(1,128)S(1)}) custom-call(bf16[4,128,8,128]{3,2,1,0:T(8,128)(2,1)} %fields_hbm.1, s32[32,8,128]{2,1,0:T(8,128)} %bracket_hbm.1, bf16[32,8,128]{2,1,0:T(8,128)(2,1)} %fraction_hbm.1), custom_call_target="tpu_custom_call" | custom-call | tf_op jit(solution)/shard_map/pallas_call | solution.py:350
  8.2 0.7 %shard_map.59 = (bf16[4,1,32,1024]{3,2,1,0:T(8,128)(2,1)}, f32[4,1,32]{2,1,0:T(1,128)}, f32[4,1,32]{2,1,0:T(1,128)}) custom-call(bf16[4,1,32,1024]{3,2,1,0:T(8,128)(2,1)S(1)} %get-tuple-element.9.rows_vmem, f32[4,1,32]{2,1,0:T(1,128)S(1)} %get-tuple-element.10.zonal_vmem, f32[4,1,32]{2,1,0:T(1,128)S(1)} %get-tuple-element.11.merid_vmem), custom_call_target="tpu_custom_call" | custom-call | tf_op jit(solution)/shard_map/pallas_call | solution.py:380

commit v4 on v3

--- a/solution.py
+++ b/solution.py
@@ -129,7 +129,8 @@
 
     for peer in peers:
         listens = jnp.logical_or(jnp.logical_or(hub, peer % 2 == 0), jnp.logical_or(peer < HUB, peer >= lon_count - 2))
-        pl.when(listens)(functools.partial(greet, peer, band))
+        apart = jnp.logical_and(far, peer < HUB)
+        pl.when(jnp.logical_and(listens, jnp.logical_not(apart)))(functools.partial(greet, peer, band))
 
     waiting = [l for l in range(lon_count - 2) if l < HUB or l % 2 == 0]
 
@@ -180,6 +181,15 @@
     def to_others(act, *args):
         for peer in peers:
             pl.when(peer >= HUB)(functools.partial(act, peer, *args))
+
+    def open_to(peer):
+        pl.semaphore_signal(go, inc=1, device_id={"lon": peer}, device_id_type=MESH)
+
+    @pl.when(far)
+    def _():
+        pl.semaphore_wait(barrier, lon_count - 1)
+        for h in range(HUB):
+            open_to(h)
 
     sums[0] = jnp.zeros((1, width), jnp.float32)
     sums[row_count + 1] = jnp.zeros((1, width), jnp.float32)
@@ -198,7 +208,7 @@
             @pl.when(early)
             def _():
                 if pair == 0 and part == 0:
-                    pl.semaphore_wait(barrier, jnp.where(far, lon_count - 1, HUB))
+                    pl.when(late)(lambda: pl.semaphore_wait(barrier, HUB))
                 send_block(0, some, pl.ds(low, count_here))
                 if pair == 0 and part == parts - 1:
                     pl.when(late)(functools.partial(send_block, 1, some))
@@ -223,35 +233,58 @@
         pl.when(up)(lambda: send_edge(row_count, 0, next_band))
         pl.when(down)(lambda: send_edge(1, lon_count - 1, prev_band))
 
-    def open_to(peer):
-        pl.semaphore_signal(go, inc=1, device_id={"lon": peer}, device_id_type=MESH)
-
-    @pl.when(full)
-    def _():
-        beyond = up.astype(jnp.int32) + down.astype(jnp.int32)
+    beyond = up.astype(jnp.int32) + down.astype(jnp.int32)
+    beside = jnp.logical_and(full, jnp.logical_not(hub))
+
+    def choose(group, act, *args):
+        for peer, aside in others:
+            distant = peer >= lon_count - 2
+            wanted = {
+                "far": distant,
+                "near": jnp.logical_not(jnp.logical_or(distant, peer < HUB)),
+                "aside": jnp.logical_and(peer >= HUB, aside),
+                "rest": jnp.logical_and(peer >= HUB, jnp.logical_not(aside)),
+            }[group]
+            pl.when(wanted)(functools.partial(act, peer, *args))
+
+    def send_edges():
+        pl.when(up)(lambda: send_edge(row_count, 0, next_band))
+        pl.when(down)(lambda: send_edge(1, lon_count - 1, prev_band))
+
+    @pl.when(hub)
+    def _():
+        pl.semaphore_wait(barrier, lon_count - 3 + beyond)
+        choose("near", send_block, whole)
+        to_hubs(send_sums)
+        choose("near", send_sums)
+        pl.when(me == 1)(functools.partial(send_block, 0, whole))
+        pl.when(me == 0)(functools.partial(send_block, 1, whole))
+        pl.semaphore_wait(go, 2)
+        send_edges()
+        choose("far", send_sums)
+        choose("far", send_block, whole)
+
+    @pl.when(beside)
+    def _():
         pl.semaphore_wait(barrier, lon_count - 1 + beyond)
-        pl.when(jnp.logical_not(hub))(lambda: open_to(me + 1))
+        open_to(me + 1)
 
         @pl.when(me == lon_count - 4)
         def _():
             open_to(lon_count - 2)
             open_to(lon_count - 1)
 
-    to_hubs(send_sums)
-
-    @pl.when(full)
-    def _():
+        to_hubs(send_sums)
         send_edges()
         to_others(send_sums)
-        pl.when(jnp.logical_not(first))(functools.partial(send_block, 0, whole))
-        for peer, aside in others:
-            pl.when(jnp.logical_and(peer >= HUB, aside))(functools.partial(send_block, peer, whole))
-        pl.when(me != 1)(functools.partial(send_block, 1, whole))
-        for peer, aside in others:
-            pl.when(jnp.logical_and(peer >= HUB, jnp.logical_not(aside)))(functools.partial(send_block, peer, whole))
+        send_block(0, whole)
+        choose("aside", send_block, whole)
+        send_block(1, whole)
+        choose("rest", send_block, whole)
 
     @pl.when(early)
     def _():
+        to_hubs(send_sums)
         for pair in range(1, pair_count):
             pl.when(late)(functools.partial(send_block, 1, pl.ds(2 * pair, 2)))
 

time: 9.07 us -> 9.07 us (level)
  no operation moved by 1% of the time
where the time goes in v4:
time: 9.07 us; the launch traced here: 8.92 us
  Pallas kernels  8.28 us (91%)
  between operations  0.64 us (7%)
    pallas_call x1, Pallas kernels, shards(): pl.pallas_call(functools.partial(exchange, lon_count, lat_count, float(lo...  7.56 us
    pallas_call x1, Pallas kernels, shards(): pl.pallas_call(finish, out_shape=(jax.ShapeDtypeStruct(rows_shape, jnp.bf...  0.72 us

profile of v4, /device:TPU:0, one launch (start us, length us, event | category | flops | bytes accessed | tf_op | source)
XLA Modules:
  0.0 8.9 jit_solution(14177056615860134591)
XLA Ops:
  0.6 7.6 %shard_map.58 = (bf16[4,1,32,1024]{3,2,1,0:T(8,128)(2,1)S(1)}, f32[4,1,32]{2,1,0:T(1,128)S(1)}, f32[4,1,32]{2,1,0:T(1,128)S(1)}) custom-call(bf16[4,128,8,128]{3,2,1,0:T(8,128)(2,1)} %fields_hbm.1, s32[32,8,128]{2,1,0:T(8,128)} %bracket_hbm.1, bf16[32,8,128]{2,1,0:T(8,128)(2,1)} %fraction_hbm.1), custom_call_target="tpu_custom_call" | custom-call | tf_op jit(solution)/shard_map/pallas_call | solution.py:383
  8.2 0.7 %shard_map.59 = (bf16[4,1,32,1024]{3,2,1,0:T(8,128)(2,1)}, f32[4,1,32]{2,1,0:T(1,128)}, f32[4,1,32]{2,1,0:T(1,128)}) custom-call(bf16[4,1,32,1024]{3,2,1,0:T(8,128)(2,1)S(1)} %get-tuple-element.9.rows_vmem, f32[4,1,32]{2,1,0:T(1,128)S(1)} %get-tuple-element.10.zonal_vmem, f32[4,1,32]{2,1,0:T(1,128)S(1)} %get-tuple-element.11.merid_vmem), custom_call_target="tpu_custom_call" | custom-call | tf_op jit(solution)/shard_map/pallas_call | solution.py:413

commit v5 on v4

--- a/solution.py
+++ b/solution.py
@@ -205,13 +205,16 @@
             low = part * count_here
             interpolate(pair, range(low, low + count_here), fields, bracket, fraction, send)
 
+            if pair == pair_count - 1 and part == parts - 1:
+                continue
+
             @pl.when(early)
             def _():
                 if pair == 0 and part == 0:
                     pl.when(late)(lambda: pl.semaphore_wait(barrier, HUB))
                 send_block(0, some, pl.ds(low, count_here))
                 if pair == 0 and part == parts - 1:
-                    pl.when(late)(functools.partial(send_block, 1, some))
+                    pl.when(jnp.logical_or(late, last))(functools.partial(send_block, 1, some))
 
     ones = jnp.ones((TILE, lons), jnp.bfloat16)
 
@@ -284,13 +287,16 @@
 
     @pl.when(early)
     def _():
-        to_hubs(send_sums)
+        send_sums(0)
+        send_block(0, some, pl.ds(low, count_here))
+        send_sums(1)
         for pair in range(1, pair_count):
             pl.when(late)(functools.partial(send_block, 1, pl.ds(2 * pair, 2)))
 
         @pl.when(far)
         def _():
-            send_block(1, whole)
+            pl.when(last)(functools.partial(send_block, 1, pl.ds(2, var_count - 2)))
+            pl.when(jnp.logical_not(last))(functools.partial(send_block, 1, whole))
             to_others(send_sums)
             to_others(send_block, whole)
 

time: 9.07 us -> 9.01 us (level)
  the two profiles are of different devices: /device:TPU:0 before, /device:TPU:1 now
where the time goes in v5:
time: 9.01 us; the launch traced here: 8.85 us
  Pallas kernels  8.22 us (91%)
  between operations  0.64 us (7%)
    pallas_call x1, Pallas kernels, shards(): pl.pallas_call(functools.partial(exchange, lon_count, lat_count, float(lo...  7.49 us
    pallas_call x1, Pallas kernels, shards(): pl.pallas_call(finish, out_shape=(jax.ShapeDtypeStruct(rows_shape, jnp.bf...  0.72 us

profile of v5, /device:TPU:1, one launch (start us, length us, event | category | flops | bytes accessed | tf_op | source)
XLA Modules:
  0.0 8.9 jit_solution(14815366177683023566)
XLA Ops:
  0.6 7.5 %shard_map.58 = (bf16[4,1,32,1024]{3,2,1,0:T(8,128)(2,1)S(1)}, f32[4,1,32]{2,1,0:T(1,128)S(1)}, f32[4,1,32]{2,1,0:T(1,128)S(1)}) custom-call(bf16[4,128,8,128]{3,2,1,0:T(8,128)(2,1)} %fields_hbm.1, s32[32,8,128]{2,1,0:T(8,128)} %bracket_hbm.1, bf16[32,8,128]{2,1,0:T(8,128)(2,1)} %fraction_hbm.1), custom_call_target="tpu_custom_call" | custom-call | tf_op jit(solution)/shard_map/pallas_call | solution.py:389
  8.1 0.7 %shard_map.59 = (bf16[4,1,32,1024]{3,2,1,0:T(8,128)(2,1)}, f32[4,1,32]{2,1,0:T(1,128)}, f32[4,1,32]{2,1,0:T(1,128)}) custom-call(bf16[4,1,32,1024]{3,2,1,0:T(8,128)(2,1)S(1)} %get-tuple-element.9.rows_vmem, f32[4,1,32]{2,1,0:T(1,128)S(1)} %get-tuple-element.10.zonal_vmem, f32[4,1,32]{2,1,0:T(1,128)S(1)} %get-tuple-element.11.merid_vmem), custom_call_target="tpu_custom_call" | custom-call | tf_op jit(solution)/shard_map/pallas_call | solution.py:419

commit v6 on v5

--- a/solution.py
+++ b/solution.py
@@ -107,7 +107,7 @@
     full = jnp.logical_not(early)
 
     get_bracket = pltpu.make_async_copy(bracket_hbm, bracket, in_sem.at[0])
-    get_fraction = pltpu.make_async_copy(fraction_hbm, fraction, in_sem.at[1])
+    get_fraction = pltpu.make_async_copy(fraction_hbm, fraction, in_sem.at[0])
     get_bracket.start()
     get_fraction.start()
 
@@ -365,10 +365,10 @@
         pltpu.make_async_copy(zonal_vmem, zonal_hbm, sem.at[1]),
         pltpu.make_async_copy(merid_vmem, merid_hbm, sem.at[2]),
     ]
+    for put in puts:
+        put.start()
     for v in range(rows_vmem.shape[0]):
         pltpu.make_async_copy(rows_vmem.at[v], out_hbm.at[v], sem.at[0]).start()
-    for put in puts:
-        put.start()
     for put in puts:
         put.wait()
     pltpu.make_async_copy(rows_vmem, out_hbm, sem.at[0]).wait()
@@ -403,7 +403,7 @@
             pltpu.VMEM((row_count + 2, 1, width), jnp.float32),
             pltpu.VMEM((lon_count, own + 2, 1, width), jnp.float32),
             pltpu.VMEM((lon_count, 1, width), jnp.float32),
-            dma((2,)),
+            dma((1,)),
             dma((var_count // 2,)),
             dma((1,)),
             dma((1,)),

time: 9.01 us -> 9 us (level)
  no operation moved by 1% of the time
where the time goes in v6:
time: 9 us; the launch traced here: 8.85 us
  Pallas kernels  8.21 us (91%)
  between operations  0.64 us (7%)
    pallas_call x1, Pallas kernels, shards(): pl.pallas_call(functools.partial(exchange, lon_count, lat_count, float(lo...  7.48 us
    pallas_call x1, Pallas kernels, shards(): pl.pallas_call(finish, out_shape=(jax.ShapeDtypeStruct(rows_shape, jnp.bf...  0.73 us

profile of v6, /device:TPU:1, one launch (start us, length us, event | category | flops | bytes accessed | tf_op | source)
XLA Modules:
  0.0 8.8 jit_solution(14737037338180489851)
XLA Ops:
  0.6 7.5 %shard_map.58 = (bf16[4,1,32,1024]{3,2,1,0:T(8,128)(2,1)S(1)}, f32[4,1,32]{2,1,0:T(1,128)S(1)}, f32[4,1,32]{2,1,0:T(1,128)S(1)}) custom-call(bf16[4,128,8,128]{3,2,1,0:T(8,128)(2,1)} %fields_hbm.1, s32[32,8,128]{2,1,0:T(8,128)} %bracket_hbm.1, bf16[32,8,128]{2,1,0:T(8,128)(2,1)} %fraction_hbm.1), custom_call_target="tpu_custom_call" | custom-call | tf_op jit(solution)/shard_map/pallas_call | solution.py:389
  8.1 0.7 %shard_map.59 = (bf16[4,1,32,1024]{3,2,1,0:T(8,128)(2,1)}, f32[4,1,32]{2,1,0:T(1,128)}, f32[4,1,32]{2,1,0:T(1,128)}) custom-call(bf16[4,1,32,1024]{3,2,1,0:T(8,128)(2,1)S(1)} %get-tuple-element.9.rows_vmem, f32[4,1,32]{2,1,0:T(1,128)S(1)} %get-tuple-element.10.zonal_vmem, f32[4,1,32]{2,1,0:T(1,128)S(1)} %get-tuple-element.11.merid_vmem), custom_call_target="tpu_custom_call" | custom-call | tf_op jit(solution)/shard_map/pallas_call | solution.py:419

commit v7 on v6

--- a/solution.py
+++ b/solution.py
@@ -362,8 +362,8 @@
 
 def finish(rows_vmem, zonal_vmem, merid_vmem, out_hbm, zonal_hbm, merid_hbm, sem):
     puts = [
-        pltpu.make_async_copy(zonal_vmem, zonal_hbm, sem.at[1]),
-        pltpu.make_async_copy(merid_vmem, merid_hbm, sem.at[2]),
+        pltpu.make_async_copy(zonal_vmem, zonal_hbm, sem.at[0]),
+        pltpu.make_async_copy(merid_vmem, merid_hbm, sem.at[0]),
     ]
     for put in puts:
         put.start()
@@ -425,7 +425,7 @@
         ),
         in_specs=[in_vmem] * 3,
         out_specs=(anywhere,) * 3,
-        scratch_shapes=[dma((3,))],
+        scratch_shapes=[dma((1,))],
         compiler_params=pltpu.CompilerParams(vmem_limit_bytes=8 << 20),
     )(*held)
     return (

time: 9 us -> 8.98 us (level)
  no operation moved by 1% of the time
where the time goes in v7:
time: 8.98 us; the launch traced here: 8.83 us
  Pallas kernels  8.19 us (91%)
  between operations  0.64 us (7%)
    pallas_call x1, Pallas kernels, shards(): pl.pallas_call(functools.partial(exchange, lon_count, lat_count, float(lo...  7.48 us
    pallas_call x1, Pallas kernels, shards(): pl.pallas_call(finish, out_shape=(jax.ShapeDtypeStruct(rows_shape, jnp.bf...  0.71 us

profile of v7, /device:TPU:1, one launch (start us, length us, event | category | flops | bytes accessed | tf_op | source)
XLA Modules:
  0.0 8.8 jit_solution(6251909355831010200)
XLA Ops:
  0.6 7.5 %shard_map.58 = (bf16[4,1,32,1024]{3,2,1,0:T(8,128)(2,1)S(1)}, f32[4,1,32]{2,1,0:T(1,128)S(1)}, f32[4,1,32]{2,1,0:T(1,128)S(1)}) custom-call(bf16[4,128,8,128]{3,2,1,0:T(8,128)(2,1)} %fields_hbm.1, s32[32,8,128]{2,1,0:T(8,128)} %bracket_hbm.1, bf16[32,8,128]{2,1,0:T(8,128)(2,1)} %fraction_hbm.1), custom_call_target="tpu_custom_call" | custom-call | tf_op jit(solution)/shard_map/pallas_call | solution.py:389
  8.1 0.7 %shard_map.59 = (bf16[4,1,32,1024]{3,2,1,0:T(8,128)(2,1)}, f32[4,1,32]{2,1,0:T(1,128)}, f32[4,1,32]{2,1,0:T(1,128)}) custom-call(bf16[4,1,32,1024]{3,2,1,0:T(8,128)(2,1)S(1)} %get-tuple-element.9.rows_vmem, f32[4,1,32]{2,1,0:T(1,128)S(1)} %get-tuple-element.10.zonal_vmem, f32[4,1,32]{2,1,0:T(1,128)S(1)} %get-tuple-element.11.merid_vmem), custom_call_target="tpu_custom_call" | custom-call | tf_op jit(solution)/shard_map/pallas_call | solution.py:419

commit v8 on v7

--- a/solution.py
+++ b/solution.py
@@ -13,7 +13,7 @@
 PACK = 16
 MESH = pl.DeviceIdType.MESH
 HUB = 2
-PARTS = (2, 2)
+PARTS = (2, 4)
 
 
 def select_pair(levels, masks):
@@ -278,9 +278,9 @@
             open_to(lon_count - 1)
 
         to_hubs(send_sums)
+        send_block(0, whole)
         send_edges()
         to_others(send_sums)
-        send_block(0, whole)
         choose("aside", send_block, whole)
         send_block(1, whole)
         choose("rest", send_block, whole)

time: 8.98 us -> 8.97 us (level)
  the two profiles are of different devices: /device:TPU:1 before, /device:TPU:0 now
where the time goes in v8:
time: 8.97 us; the launch traced here: 8.81 us
  Pallas kernels  8.17 us (91%)
  between operations  0.64 us (7%)
    pallas_call x1, Pallas kernels, shards(): pl.pallas_call(functools.partial(exchange, lon_count, lat_count, float(lo...  7.46 us
    pallas_call x1, Pallas kernels, shards(): pl.pallas_call(finish, out_shape=(jax.ShapeDtypeStruct(rows_shape, jnp.bf...  0.71 us

profile of v8, /device:TPU:0, one launch (start us, length us, event | category | flops | bytes accessed | tf_op | source)
XLA Modules:
  0.0 8.8 jit_solution(9140766383005365173)
XLA Ops:
  0.6 7.5 %shard_map.58 = (bf16[4,1,32,1024]{3,2,1,0:T(8,128)(2,1)S(1)}, f32[4,1,32]{2,1,0:T(1,128)S(1)}, f32[4,1,32]{2,1,0:T(1,128)S(1)}) custom-call(bf16[4,128,8,128]{3,2,1,0:T(8,128)(2,1)} %fields_hbm.1, s32[32,8,128]{2,1,0:T(8,128)} %bracket_hbm.1, bf16[32,8,128]{2,1,0:T(8,128)(2,1)} %fraction_hbm.1), custom_call_target="tpu_custom_call" | custom-call | tf_op jit(solution)/shard_map/pallas_call | solution.py:389
  8.1 0.7 %shard_map.59 = (bf16[4,1,32,1024]{3,2,1,0:T(8,128)(2,1)}, f32[4,1,32]{2,1,0:T(1,128)}, f32[4,1,32]{2,1,0:T(1,128)}) custom-call(bf16[4,1,32,1024]{3,2,1,0:T(8,128)(2,1)S(1)} %get-tuple-element.9.rows_vmem, f32[4,1,32]{2,1,0:T(1,128)S(1)} %get-tuple-element.10.zonal_vmem, f32[4,1,32]{2,1,0:T(1,128)S(1)} %get-tuple-element.11.merid_vmem), custom_call_target="tpu_custom_call" | custom-call | tf_op jit(solution)/shard_map/pallas_call | solution.py:419

commit v9 on v8

--- a/solution.py
+++ b/solution.py
@@ -278,9 +278,9 @@
             open_to(lon_count - 1)
 
         to_hubs(send_sums)
-        send_block(0, whole)
         send_edges()
         to_others(send_sums)
+        send_block(0, whole)
         choose("aside", send_block, whole)
         send_block(1, whole)
         choose("rest", send_block, whole)

time: 8.97 us -> 8.97 us (level)
  no operation moved by 1% of the time
where the time goes in v9:
time: 8.97 us; the launch traced here: 8.81 us
  Pallas kernels  8.17 us (91%)
  between operations  0.64 us (7%)
    pallas_call x1, Pallas kernels, shards(): pl.pallas_call(functools.partial(exchange, lon_count, lat_count, float(lo...  7.46 us
    pallas_call x1, Pallas kernels, shards(): pl.pallas_call(finish, out_shape=(jax.ShapeDtypeStruct(rows_shape, jnp.bf...  0.71 us

profile of v9, /device:TPU:0, one launch (start us, length us, event | category | flops | bytes accessed | tf_op | source)
XLA Modules:
  0.0 8.8 jit_solution(2492764588602811748)
XLA Ops:
  0.6 7.5 %shard_map.58 = (bf16[4,1,32,1024]{3,2,1,0:T(8,128)(2,1)S(1)}, f32[4,1,32]{2,1,0:T(1,128)S(1)}, f32[4,1,32]{2,1,0:T(1,128)S(1)}) custom-call(bf16[4,128,8,128]{3,2,1,0:T(8,128)(2,1)} %fields_hbm.1, s32[32,8,128]{2,1,0:T(8,128)} %bracket_hbm.1, bf16[32,8,128]{2,1,0:T(8,128)(2,1)} %fraction_hbm.1), custom_call_target="tpu_custom_call" | custom-call | tf_op jit(solution)/shard_map/pallas_call | solution.py:389
  8.1 0.7 %shard_map.59 = (bf16[4,1,32,1024]{3,2,1,0:T(8,128)(2,1)}, f32[4,1,32]{2,1,0:T(1,128)}, f32[4,1,32]{2,1,0:T(1,128)}) custom-call(bf16[4,1,32,1024]{3,2,1,0:T(8,128)(2,1)S(1)} %get-tuple-element.9.rows_vmem, f32[4,1,32]{2,1,0:T(1,128)S(1)} %get-tuple-element.10.zonal_vmem, f32[4,1,32]{2,1,0:T(1,128)S(1)} %get-tuple-element.11.merid_vmem), custom_call_target="tpu_custom_call" | custom-call | tf_op jit(solution)/shard_map/pallas_call | solution.py:419
